TPU v7x, 32 devices: a whole 2x2x4 slice. The times are simulated.
32 devices in a mesh: groups: 2 (over x), feat: 16 (over z, y, core).
Axes of the slice: x: 2, y: 2, z: 4, core: 2. Of those that a mesh axis runs over, the one named last changes fastest.
Arguments:
- cells: bfloat16 [96, 512, 192], P('groups', 'feat'), parts along dimension 0, may hold values from -6 to 6
- missing: int32 [96, 512], P('groups', 'feat'), parts along dimension 0, may hold values 0 or 1
- feat_ids: int32 [1024], P(('groups', 'feat')), parts along dimension 0, may hold values from 0 to 63
- feat_table: float32 [64, 192], replicated, may hold values from -5 to 5
- nan_embed: float32 [192], replicated, may hold values from -5 to 5
- gain_one: float32 [192], replicated, may hold values from 0.1 to 1.9
- w_qkv: bfloat16 [192, 576], replicated, may hold values from -3 to 3
- w_out: bfloat16 [192, 192], replicated, may hold values from -0.4375 to 0.4375
- gain_two: float32 [192], replicated, may hold values from 0.1 to 1.9
- w_up: bfloat16 [192, 768], replicated, may hold values from -0.4375 to 0.4375
- w_down: bfloat16 [768, 192], replicated, may hold values from -0.21875 to 0.21875
Outputs:
- result: float32 [96, 512, 192], P('groups', 'feat'), parts along dimension 0
There are 2 independent parts, one for each index of `groups`. A program takes and returns all parts, laid end to end along the dimension named above; an argument that names none is the same for every part. Nothing has to cross between parts.
All inputs are finite; a program needn't handle non-finite values. No bound on the sum of `missing` on one device may be relied on, other than what follows from the above.
Results may differ from a plain program's by a relative error of at most 0.007.
The roundings to bfloat16 on the way count: a program that leaves them out, or rounds other values in their place, can miss the bound.
Values may be sent and summed in bfloat16 or wider, within the bound.
A program may use at most 64 MiB of HBM per device.

v0:
```python
import jax
import jax.numpy as jnp
from jax import lax
from jax.sharding import PartitionSpec as P

HEADS = 6


def cell_norm(values, gain):
    mean = jnp.mean(values, axis=-1, keepdims=True)
    centered = values - mean
    var = jnp.mean(centered * centered, axis=-1, keepdims=True)
    return centered * lax.rsqrt(var + 1e-05) * gain


def attend(qkv):
    width = qkv.shape[-1] // 3
    count = qkv.shape[0]
    head_dim = width // HEADS
    query = qkv[:, :width].reshape(count, HEADS, head_dim)
    keys = qkv[:, width : 2 * width].reshape(count, HEADS, head_dim)
    values = qkv[:, 2 * width :].reshape(count, HEADS, head_dim)
    scores = jnp.einsum(
        "qhd,phd->hqp", query, keys, preferred_element_type=jnp.float32
    ) * head_dim ** (-0.5)
    top = jnp.max(scores, axis=-1, keepdims=True)
    expo = jnp.exp(scores - top)
    probs = (expo / jnp.sum(expo, axis=-1, keepdims=True)).astype(jnp.bfloat16)
    context = jnp.einsum("hqp,phd->qhd", probs, values, preferred_element_type=jnp.float32)
    return context.astype(jnp.bfloat16).reshape(count, width)


def finish(base, context, w_out, gain_two, w_up, w_down):
    mid = base + jnp.dot(context, w_out, preferred_element_type=jnp.float32)
    normed_two = cell_norm(mid, gain_two).astype(jnp.bfloat16)
    act = jax.nn.gelu(
        jnp.dot(normed_two, w_up, preferred_element_type=jnp.float32), approximate=False
    ).astype(jnp.bfloat16)
    return mid + jnp.dot(act, w_down, preferred_element_type=jnp.float32)


def body(
    cells, missing, feat_ids, feat_table, nan_embed, gain_one, w_qkv, w_out, gain_two, w_up, w_down
):
    devices = lax.axis_size("feat")
    all_rows, local_feats, width = cells.shape
    onehot = (
        feat_ids[:, None] == jnp.arange(feat_table.shape[0], dtype=jnp.int32)[None, :]
    ).astype(jnp.float32)
    femb = jnp.dot(onehot, feat_table, precision=lax.Precision.HIGHEST)
    tokens = (
        cells.astype(jnp.float32) + missing[..., None].astype(jnp.float32) * nan_embed + femb[None]
    ).astype(jnp.bfloat16)

    def one_row(row):
        base = row.astype(jnp.float32)
        normed = cell_norm(base, gain_one).astype(jnp.bfloat16)
        qkv = jnp.dot(normed, w_qkv, preferred_element_type=jnp.float32).astype(jnp.bfloat16)
        return finish(base, attend(qkv), w_out, gain_two, w_up, w_down)

    grouped = tokens.reshape(devices, all_rows // devices, local_feats, width)
    outputs = lax.map(
        one_row, lax.all_to_all(grouped, "feat", split_axis=0, concat_axis=2, tiled=True)[0]
    )
    back = lax.all_to_all(outputs[None], "feat", split_axis=2, concat_axis=0, tiled=True)
    return back.reshape(all_rows, local_feats, width)


def solution(mesh):
    in_specs = (
        P("groups", "feat", None),
        P("groups", "feat"),
        P(("groups", "feat")),
        P(),
        P(),
        P(),
        P(),
        P(),
        P(),
        P(),
        P(),
    )
    out_specs = P("groups", "feat", None)
    return jax.shard_map(body, mesh=mesh, in_specs=in_specs, out_specs=out_specs, check_vma=False)
```

profile of v0, /device:TPU:0, one launch (start us, length us, event | category | flops | bytes accessed | tf_op | source)
XLA Modules:
  0.0 114.5 jit_solution(52728647301526461)
XLA Ops:
  0.0 0.8 convert_element_type.39
  0.8 0.9 fusion.102
  1.7 2.4 %add_convert_fusion = bf16[48,32,192]{2,1,0:T(8,128)(2,1)} fusion(bf16[48,32,192]{2,1,0:T(8,128)(2,1)} %param.13, f32[32,192]{1,0:T(8,128)S(1)} %fusion.102, f32[192]{0:T(256)} %param.17, f32[48,32]{1,0:T(8,128)S(1)} %copy.42), kind=kLoop, calls=%fused_computation.117 | loop fusion | flops 1474560 | bytes 1211136 | tf_op jit(solution)/shard_map/convert_element_type | solution.py:53
  4.1 7.4 %all-to-all-start = ((bf16[16,3,32,192]{3,2,1,0:T(8,128)(2,1)}), bf16[16,3,32,192]{3,2,1,0:T(8,128)(2,1)S(1)}, u32[]{:S(2)}, u32[]{:S(2)}) async-start(bf16[16,3,32,192]{3,2,1,0:T(8,128)(2,1)} %bitcast.7), calls=%async_computation | async-start | bytes 1572864 | tf_op jit(solution)/shard_map/all_to_all | solution.py:63
  11.5 18.6 %all-to-all-done = bf16[16,3,32,192]{3,2,1,0:T(8,128)(2,1)S(1)} async-done(((bf16[16,3,32,192]{3,2,1,0:T(8,128)(2,1)}), bf16[16,3,32,192]{3,2,1,0:T(8,128)(2,1)S(1)}, u32[]{:S(2)}, u32[]{:S(2)}) %all-to-all-start) | async-done | bytes 589856 | tf_op jit(solution)/shard_map/all_to_all | solution.py:63
  30.5 40.1 %while.10 = (s32[]{:T(128)}, f32[3,512,192]{1,2,0:T(8,128)S(1)}, bf16[3,512,192]{1,2,0:T(8,128)(2,1)S(1)}, f32[192]{0:T(256)S(1)}, bf16[192,576]{1,0:T(8,128)(2,...) while((s32[]{:T(128)}, f32[3,512,192]{1,2,0:T(8,128)S(1)}, ...), condition=%wide.region_7.8_spmd, body=%wide.region_0.7_spmd.sunk | while | flops 690292224 | bytes 21420208 | solution.py:62
  30.7 0.4 convolution_convert_fusion.2
  31.2 4.8 %fusion.144 = (f32[6,512]{1,0:T(8,128)S(1)}, f32[6,512,512]{1,2,0:T(8,128)}) fusion(bf16[512,6,32]{0,2,1:T(8,128)(2,1)S(1)} %bitcast.81, bf16[512,6,32]{0,2,1:T(8,128)(2,1)S(1)} %bitcast.80), kind=kOutput, calls=%fused_computation.122.clone.1 | convolution fusion | flops 105382400 | bytes 6696960 | tf_op jit(solution)/shard_map/while/body/eval_jaxpr/sub | solution.py:27
  35.9 3.5 %fusion.145 = bf16[6,32,512]{2,1,0:T(8,128)(2,1)S(1)} fusion(bf16[512,6,32]{0,2,1:T(8,128)(2,1)S(1)} %bitcast.79, f32[6,512,512]{1,2,0:T(8,128)} %get-tuple-element.188, f32[6,512]{1,0:T(8,128)S(1)} %get-tuple-element.189), kind=kOutput, calls=%fused_computation.32.clone.1 | convolution fusion | flops 103907328 | bytes 6696960 | tf_op jit(solution)/shard_map/while/body/eval_jaxpr/hqp,phd->qhd/dot_general | solution.py:29
  39.4 0.3 fusion.146
  39.8 4.1 %fusion.147 = f32[3,512,192]{1,2,0:T(8,128)S(1)} fusion(f32[3,512,192]{1,2,0:T(8,128)S(1)} %get-tuple-element.203, s32[]{:T(128)} %get-tuple-element.202, f32[512,192]{0,1:T(8,128)S(1)} %get-tuple-element.190, bf16[768,192]{0,1:T(8,128)(2,1)S(1)} %copy-done.5, bf16[192,768]{1,0:T(8,128)(2,1)S(1)} %copy-done.4, f32[192]{0:T(256)S(1)} %get-tuple-element.218, ...), kind=kOutput, calls=%fused_computation.31.clone.1 | convolution fusion | flops 328040448 | bytes 1774596 | tf_op jit(solution)/shard_map/while/body/eval_jaxpr/dot_general | solution.py:39
  44.1 0.4 convolution_convert_fusion.2
  44.5 4.8 %fusion.144 = (f32[6,512]{1,0:T(8,128)S(1)}, f32[6,512,512]{1,2,0:T(8,128)}) fusion(bf16[512,6,32]{0,2,1:T(8,128)(2,1)S(1)} %bitcast.81, bf16[512,6,32]{0,2,1:T(8,128)(2,1)S(1)} %bitcast.80), kind=kOutput, calls=%fused_computation.122.clone.1 | convolution fusion | flops 105382400 | bytes 6696960 | tf_op jit(solution)/shard_map/while/body/eval_jaxpr/sub | solution.py:27
  49.3 3.5 %fusion.145 = bf16[6,32,512]{2,1,0:T(8,128)(2,1)S(1)} fusion(bf16[512,6,32]{0,2,1:T(8,128)(2,1)S(1)} %bitcast.79, f32[6,512,512]{1,2,0:T(8,128)} %get-tuple-element.188, f32[6,512]{1,0:T(8,128)S(1)} %get-tuple-element.189), kind=kOutput, calls=%fused_computation.32.clone.1 | convolution fusion | flops 103907328 | bytes 6696960 | tf_op jit(solution)/shard_map/while/body/eval_jaxpr/hqp,phd->qhd/dot_general | solution.py:29
  52.8 0.3 fusion.146
  53.2 4.1 %fusion.147 = f32[3,512,192]{1,2,0:T(8,128)S(1)} fusion(f32[3,512,192]{1,2,0:T(8,128)S(1)} %get-tuple-element.203, s32[]{:T(128)} %get-tuple-element.202, f32[512,192]{0,1:T(8,128)S(1)} %get-tuple-element.190, bf16[768,192]{0,1:T(8,128)(2,1)S(1)} %copy-done.5, bf16[192,768]{1,0:T(8,128)(2,1)S(1)} %copy-done.4, f32[192]{0:T(256)S(1)} %get-tuple-element.218, ...), kind=kOutput, calls=%fused_computation.31.clone.1 | convolution fusion | flops 328040448 | bytes 1774596 | tf_op jit(solution)/shard_map/while/body/eval_jaxpr/dot_general | solution.py:39
  57.4 0.4 convolution_convert_fusion.2
  57.9 4.8 %fusion.144 = (f32[6,512]{1,0:T(8,128)S(1)}, f32[6,512,512]{1,2,0:T(8,128)}) fusion(bf16[512,6,32]{0,2,1:T(8,128)(2,1)S(1)} %bitcast.81, bf16[512,6,32]{0,2,1:T(8,128)(2,1)S(1)} %bitcast.80), kind=kOutput, calls=%fused_computation.122.clone.1 | convolution fusion | flops 105382400 | bytes 6696960 | tf_op jit(solution)/shard_map/while/body/eval_jaxpr/sub | solution.py:27
  62.7 3.5 %fusion.145 = bf16[6,32,512]{2,1,0:T(8,128)(2,1)S(1)} fusion(bf16[512,6,32]{0,2,1:T(8,128)(2,1)S(1)} %bitcast.79, f32[6,512,512]{1,2,0:T(8,128)} %get-tuple-element.188, f32[6,512]{1,0:T(8,128)S(1)} %get-tuple-element.189), kind=kOutput, calls=%fused_computation.32.clone.1 | convolution fusion | flops 103907328 | bytes 6696960 | tf_op jit(solution)/shard_map/while/body/eval_jaxpr/hqp,phd->qhd/dot_general | solution.py:29
  66.2 0.3 fusion.146
  66.6 4.1 %fusion.147 = f32[3,512,192]{1,2,0:T(8,128)S(1)} fusion(f32[3,512,192]{1,2,0:T(8,128)S(1)} %get-tuple-element.203, s32[]{:T(128)} %get-tuple-element.202, f32[512,192]{0,1:T(8,128)S(1)} %get-tuple-element.190, bf16[768,192]{0,1:T(8,128)(2,1)S(1)} %copy-done.5, bf16[192,768]{1,0:T(8,128)(2,1)S(1)} %copy-done.4, f32[192]{0:T(256)S(1)} %get-tuple-element.218, ...), kind=kOutput, calls=%fused_computation.31.clone.1 | convolution fusion | flops 328040448 | bytes 1774596 | tf_op jit(solution)/shard_map/while/body/eval_jaxpr/dot_general | solution.py:39
  70.6 1.4 %copy.45 = f32[1,3,512,192]{3,0,1,2:T(1,128)S(1)} copy(f32[1,3,512,192]{2,3,1,0:T(8,128)S(1)} %bitcast.85) | data formatting | bytes 2359296 | tf_op jit(solution)/shard_map/broadcast_in_dim | solution.py:65
  72.0 41.1 %all_to_all.30 = f32[1,3,512,192]{3,0,1,2:T(1,128)S(1)} all-to-all(f32[1,3,512,192]{3,0,1,2:T(1,128)S(1)} %copy.45), channel_id=1, replica_groups=mesh['groups'=2,'feat'=16] {'feat'}, dimensions={2} | all-to-all | bytes 2359296 | tf_op jit(solution)/shard_map/all_to_all | solution.py:65
  113.2 1.3 %copy.47 = f32[16,1,3,32,192]{4,3,2,0,1:T(8,128)} copy(f32[16,1,3,32,192]{4,3,0,2,1:T(8,128)S(1)} %bitcast.78) | data formatting | bytes 2359296 | tf_op jit(solution)/shard_map/all_to_all | solution.py:65
  (51 shorter events, 1.4 us)
Async XLA Ops:
  0.0 0.8 copy-start
  4.1 26.1 %all-to-all-start = ((bf16[16,3,32,192]{3,2,1,0:T(8,128)(2,1)}), bf16[16,3,32,192]{3,2,1,0:T(8,128)(2,1)S(1)}, u32[]{:S(2)}, u32[]{:S(2)}) async-start(bf16[16,3,32,192]{3,2,1,0:T(8,128)(2,1)} %bitcast.7), calls=%async_computation | async-start | bytes 1572864 | tf_op jit(solution)/shard_map/all_to_all | solution.py:63
  11.5 19.0 %copy-start.1 = (bf16[192,576]{1,0:T(8,128)(2,1)S(1)}, bf16[192,576]{1,0:T(8,128)(2,1)}, u32[]{:S(2)}) copy-start(bf16[192,576]{1,0:T(8,128)(2,1)} %param.19) | copy-start | bytes 663556
  11.5 19.0 %copy-start.2 = (bf16[192,192]{1,0:T(8,128)(2,1)S(1)}, bf16[192,192]{1,0:T(8,128)(2,1)}, u32[]{:S(2)}) copy-start(bf16[192,192]{1,0:T(8,128)(2,1)} %param.20) | copy-start | bytes 221188
  11.5 19.0 %copy-start.3 = (f32[192]{0:T(256)S(1)}, f32[192]{0:T(256)}, u32[]{:S(2)}) copy-start(f32[192]{0:T(256)} %param.18) | copy-start | bytes 2308
  11.5 19.0 %copy-start.6 = (f32[192]{0:T(256)S(1)}, f32[192]{0:T(256)}, u32[]{:S(2)}) copy-start(f32[192]{0:T(256)} %param.21) | copy-start | bytes 2308
  35.9 3.9 %copy-start.4 = (bf16[192,768]{1,0:T(8,128)(2,1)S(1)}, bf16[192,768]{1,0:T(8,128)(2,1)}, u32[]{:S(2)}) copy-start(bf16[192,768]{1,0:T(8,128)(2,1)} %get-tuple-element.219) | copy-start | bytes 884740 | tf_op jit(solution)/shard_map/while
  35.9 3.9 %copy-start.5 = (bf16[768,192]{0,1:T(8,128)(2,1)S(1)}, bf16[768,192]{0,1:T(8,128)(2,1)}, u32[]{:S(2)}) copy-start(bf16[768,192]{0,1:T(8,128)(2,1)} %get-tuple-element.220) | copy-start | bytes 884740 | tf_op jit(solution)/shard_map/while
  49.3 3.9 %copy-start.4 = (bf16[192,768]{1,0:T(8,128)(2,1)S(1)}, bf16[192,768]{1,0:T(8,128)(2,1)}, u32[]{:S(2)}) copy-start(bf16[192,768]{1,0:T(8,128)(2,1)} %get-tuple-element.219) | copy-start | bytes 884740 | tf_op jit(solution)/shard_map/while
  49.3 3.9 %copy-start.5 = (bf16[768,192]{0,1:T(8,128)(2,1)S(1)}, bf16[768,192]{0,1:T(8,128)(2,1)}, u32[]{:S(2)}) copy-start(bf16[768,192]{0,1:T(8,128)(2,1)} %get-tuple-element.220) | copy-start | bytes 884740 | tf_op jit(solution)/shard_map/while
  62.7 3.9 %copy-start.4 = (bf16[192,768]{1,0:T(8,128)(2,1)S(1)}, bf16[192,768]{1,0:T(8,128)(2,1)}, u32[]{:S(2)}) copy-start(bf16[192,768]{1,0:T(8,128)(2,1)} %get-tuple-element.219) | copy-start | bytes 884740 | tf_op jit(solution)/shard_map/while
  62.7 3.9 %copy-start.5 = (bf16[768,192]{0,1:T(8,128)(2,1)S(1)}, bf16[768,192]{0,1:T(8,128)(2,1)}, u32[]{:S(2)}) copy-start(bf16[768,192]{0,1:T(8,128)(2,1)} %get-tuple-element.220) | copy-start | bytes 884740 | tf_op jit(solution)/shard_map/while
where the time goes:
time: 115 us
  blocking collectives  41.1 us (36%)
  matrix products  39.9 us (35%)
  waiting for transfers between devices  18.6 us (16%)
  starting transfers between devices  7.41 us (6%)
  other arithmetic  3.81 us (3%)
  local copies, waits for them, and re-layouts  3.3 us (3%)
    all_to_all x1, blocking collectives, body(): lax.all_to_all(outputs[None], 'feat', split_axis=2, concat_axis=0, tiled=...  41.1 us
    all_to_all x1, waiting for transfers between devices, body(): lax.all_to_all(grouped, 'feat', split_axis=0, concat_axis=2, tiled=True)[0]  18.6 us
    sub x3, matrix products, attend(): expo = jnp.exp(scores - top)  14.3 us
    dot_general x3, matrix products, finish(): return mid + jnp.dot(act, w_down, preferred_element_type=jnp.float32)  12.2 us
    dot_general x3, matrix products, attend(): jnp.einsum('hqp,phd->qhd', probs, values, preferred_element_type=jnp.floa...  10.5 us
    all_to_all x1, starting transfers between devices, body(): lax.all_to_all(grouped, 'feat', split_axis=0, concat_axis=2, tiled=True)[0]  7.41 us
    convert_element_type x1, other arithmetic, body(): tokens = (cells.astype(jnp.float32) + missing[..., None].astype(jnp.float...  2.36 us
  transfers between devices with their start and end apart: 1, of which 1 were waited for; matrix products, arithmetic and copies ran while one was open for 0% of the time, Pallas kernels for 0%

commit v1 on v0

v1 whole, which is shorter than its diff:
```python
import functools
import math

import jax
import jax.numpy as jnp
from jax import lax
from jax.experimental import pallas as pl
from jax.experimental.pallas import tpu as pltpu
from jax.sharding import PartitionSpec as P

HEADS = 6
MESH = pl.DeviceIdType.MESH
F32 = jnp.float32
BF16 = jnp.bfloat16


def cell_norm(values, gain):
    mean = jnp.mean(values, axis=-1, keepdims=True)
    centered = values - mean
    var = jnp.mean(centered * centered, axis=-1, keepdims=True)
    return (centered * lax.rsqrt(var + 1e-05) * gain).astype(BF16)


def pack(values, packed):
    if not packed:
        return values
    half = values.shape[-2] // 2
    tail = values[..., 128:]
    tail = jnp.concatenate([tail[..., :half, :], tail[..., half:, :]], axis=-1)
    return jnp.concatenate([values[..., :128], tail], axis=-2)


def unpack(values, feats, width, packed):
    if packed:
        rest = width - 128
        tail = values[:, feats:]
        tail = jnp.concatenate([tail[..., :rest], tail[..., rest:]], axis=-2)
        values = jnp.concatenate([values[:, :feats], tail], axis=-1)
    return values.reshape(values.shape[0] * feats, width)


def attend(normed, wk, wqv_t):
    width = wk.shape[0]
    head_dim = width // HEADS
    count = normed.shape[0]
    keys = jnp.dot(normed, wk, preferred_element_type=F32).astype(BF16)
    turned = lax.dot_general(
        wqv_t, normed, (((1,), (1,)), ((), ())), preferred_element_type=F32
    ).astype(BF16)
    scale = head_dim ** (-0.5) * math.log2(math.e)
    ones = jnp.ones((16, count), BF16)
    outs = []
    for head in range(HEADS):
        low = head * head_dim
        block = low // 128 * 128
        high = min(block + 128, width)
        parts = []
        if low > block:
            parts.append(jnp.zeros((low - block, count), BF16))
        parts.append(turned[low : low + head_dim])
        if high > low + head_dim:
            parts.append(jnp.zeros((high - low - head_dim, count), BF16))
        query = jnp.concatenate(parts, axis=0)
        scores = jnp.dot(keys[:, block:high], query, preferred_element_type=F32)
        top = jnp.max(scores, axis=0, keepdims=True)
        expo = jnp.exp2((scores - top) * scale).astype(BF16)
        values = jnp.concatenate([turned[width + low : width + low + head_dim], ones], axis=0)
        sums = jnp.dot(values, expo, preferred_element_type=F32)
        outs.append(sums[:head_dim] / sums[head_dim : head_dim + 1])
    return jnp.concatenate(outs, axis=0).T


def kernel(
    n, rows, feats, width, packed,
    cells, missing, feat_ids, feat_table, nan_embed, gain_one, w_qkv, w_out, gain_two, w_up, w_down,
    out, tok, got, ctx, back, wqv_t, send_sems, recv_sems,
):
    me = lax.axis_index("feat")
    barrier = pltpu.get_barrier_semaphore()

    def greet(step, carry):
        peer = lax.rem(me + step, n)
        pl.semaphore_signal(barrier, inc=1, device_id={"feat": peer}, device_id_type=MESH)
        return carry

    lax.fori_loop(1, n, greet, 0)

    ncat = feat_table.shape[0]
    hot = (lax.broadcasted_iota(jnp.int32, (ncat, feats), 0) == feat_ids[...]).astype(F32)
    femb = lax.dot_general(
        hot, feat_table[...], (((0,), (0,)), ((), ())),
        precision=lax.Precision.HIGHEST, preferred_element_type=F32,
    )
    nan = nan_embed[...]
    absent = missing[...].astype(F32)[:, :, None].reshape(n, rows, feats, 1)
    for row in range(rows):
        values = cells[:, row].astype(F32)
        values = (values + absent[:, row] * nan[None] + femb[None]).astype(BF16)
        tok[row] = pack(values, packed)

    pl.semaphore_wait(barrier, n - 1)

    def spread(source, target, kind, row):
        def one(step, carry):
            peer = lax.rem(me + step, n)
            pltpu.make_async_remote_copy(
                src_ref=source.at[row, peer],
                dst_ref=target.at[row, me],
                send_sem=send_sems.at[kind, row],
                recv_sem=recv_sems.at[kind, row],
                device_id={"feat": peer},
                device_id_type=MESH,
            ).start()
            return carry

        lax.fori_loop(1, n, one, 0)

    def settle(ref, sems, kind, row):
        piece = ref.at[row, pl.ds(0, n - 1)]
        pltpu.make_async_copy(piece, piece, sems.at[kind, row]).wait()

    for row in range(rows):
        spread(tok, got, 0, row)
    for row in range(rows):
        got[row, pl.ds(me, 1)] = tok[row, pl.ds(me, 1)]
    wqv_t[0:width] = w_qkv[:, :width].astype(F32).T.astype(BF16)
    wqv_t[width:] = w_qkv[:, 2 * width :].astype(F32).T.astype(BF16)

    def attention(row, carry):
        settle(got, recv_sems, 0, row)
        base = unpack(got[row].astype(F32), feats, width, packed)
        normed = cell_norm(base, gain_one[...])
        context = attend(normed, w_qkv[:, width : 2 * width], wqv_t[...])
        sent = pack(context.reshape(n, feats, width), packed).astype(BF16)
        ctx[row] = sent
        spread(ctx, back, 1, row)
        back[row, pl.ds(me, 1)] = ctx[row, pl.ds(me, 1)]
        return carry

    lax.fori_loop(0, rows, attention, 0)

    def finish(row, carry):
        settle(back, recv_sems, 1, row)
        context = unpack(back[row].astype(F32), feats, width, packed).astype(BF16)
        base = unpack(tok[row].astype(F32), feats, width, packed)
        mid = base + jnp.dot(context, w_out[...], preferred_element_type=F32)
        normed = cell_norm(mid, gain_two[...])
        hidden = jnp.dot(normed, w_up[...], preferred_element_type=F32)
        act = (0.5 * hidden * (1.0 + lax.erf(hidden * math.sqrt(0.5)))).astype(BF16)
        result = mid + jnp.dot(act, w_down[...], preferred_element_type=F32)
        out[:, pl.ds(row, 1)] = result.reshape(n, 1, feats, width)
        return carry

    lax.fori_loop(0, rows, finish, 0)

    for row in range(rows):
        settle(tok, send_sems, 0, row)
        settle(ctx, send_sems, 1, row)


def body(
    cells, missing, feat_ids, feat_table, nan_embed, gain_one, w_qkv, w_out, gain_two, w_up, w_down
):
    n = lax.axis_size("feat")
    all_rows, feats, width = cells.shape
    rows = all_rows // n
    packed = width == 192 and feats % 32 == 0
    piece = (feats + feats // 2, 128) if packed else (feats, width)
    buffer = pltpu.VMEM((rows, n) + piece, BF16)
    result = pl.pallas_call(
        functools.partial(kernel, n, rows, feats, width, packed),
        out_shape=jax.ShapeDtypeStruct((n, rows, feats, width), F32),
        in_specs=[pl.BlockSpec(memory_space=pltpu.VMEM)] * 11,
        out_specs=pl.BlockSpec(memory_space=pltpu.VMEM),
        scratch_shapes=[
            buffer,
            buffer,
            buffer,
            buffer,
            pltpu.VMEM((2 * width, width), BF16),
            pltpu.SemaphoreType.DMA((2, rows)),
            pltpu.SemaphoreType.DMA((2, rows)),
        ],
        compiler_params=pltpu.CompilerParams(
            collective_id=0, has_side_effects=True, vmem_limit_bytes=60 * 1024 * 1024
        ),
    )(
        cells.reshape(n, rows, feats, width),
        missing,
        feat_ids[None],
        feat_table,
        nan_embed[None],
        gain_one[None],
        w_qkv,
        w_out,
        gain_two[None],
        w_up,
        w_down,
    )
    return result.reshape(all_rows, feats, width)


def solution(mesh):
    in_specs = (
        P("groups", "feat", None),
        P("groups", "feat"),
        P(("groups", "feat")),
        P(),
        P(),
        P(),
        P(),
        P(),
        P(),
        P(),
        P(),
    )
    out_specs = P("groups", "feat", None)
    return jax.shard_map(body, mesh=mesh, in_specs=in_specs, out_specs=out_specs, check_vma=False)
```

time: 115 us -> 41.6 us (0.36)
  blocking collectives: 41.1 us -> 0 us
  matrix products: 39.9 us -> 0 us
  Pallas kernels: 0 us -> 35.3 us
  waiting for transfers between devices: 18.6 us -> 0 us
  starting transfers between devices: 7.41 us -> 0 us
  other arithmetic: 3.81 us -> 0 us
  local copies, waits for them, and re-layouts: 3.3 us -> 6 us
    all_to_all x1 -> x0, blocking collectives: 41.1 us -> none  [body(): lax.all_to_all(outputs[None], 'feat', split_axis=2, concat_axis=0, tiled=...]
    pallas_call x0 -> x1, Pallas kernels: none -> 35.3 us  [body(): pl.pallas_call(functools.partial(kernel, n, rows, feats, width, packed),...]
    dot_general x13 -> x0, matrix products: 25.6 us -> none  [the longest x3 12.2 us: finish(): return mid + jnp.dot(act, w_down, preferred_element_type=jnp.float32)]
    all_to_all x1 -> x0, waiting for transfers between devices: 18.6 us -> none  [body(): lax.all_to_all(grouped, 'feat', split_axis=0, concat_axis=2, tiled=True)[0]]
    sub x3 -> x0, matrix products: 14.3 us -> none  [attend(): expo = jnp.exp(scores - top)]
    all_to_all x1 -> x0, starting transfers between devices: 7.41 us -> none  [body(): lax.all_to_all(grouped, 'feat', split_axis=0, concat_axis=2, tiled=True)[0]]
    unnamed x10 -> x3, local copies, waits for them, and re-layouts: 0.03 us -> 6 us
    convert_element_type x2 -> x0, other arithmetic: 3.12 us -> none  [the longest x1 2.36 us: body(): tokens = (cells.astype(jnp.float32) + missing[..., None].astype(jnp.float...]
  transfers between devices with their start and end apart: 1 -> 0, of which waited for: 1 -> 0; matrix products, arithmetic and copies ran while one was open for 0% -> 0% of each run, Pallas kernels for 0% -> 0%
where the time goes in v1:
time: 41.6 us; the launch traced here: 41.3 us
  Pallas kernels  35.3 us (85%)
  local copies, waits for them, and re-layouts  6 us (14%)
    pallas_call x1, Pallas kernels, body(): pl.pallas_call(functools.partial(kernel, n, rows, feats, width, packed),...  35.3 us
    unnamed x3, local copies, waits for them, and re-layouts  6 us

profile of v1, /device:TPU:0, one launch (start us, length us, event | category | flops | bytes accessed | tf_op | source)
XLA Modules:
  0.0 41.3 jit_solution(7797101393932487906)
XLA Ops:
  0.0 1.4 %copy.12.missing = s32[48,32]{1,0:T(8,128)} copy(s32[48,32]{0,1:T(8,128)} %param.12) | data formatting | bytes 12288 | tf_op args[1]
  1.4 1.9 %copy.13.w_down = bf16[768,192]{1,0:T(8,128)(2,1)} copy(bf16[768,192]{0,1:T(8,128)(2,1)} %param.21) | data formatting | bytes 589824 | tf_op args[10]
  3.3 35.3 %shard_map.109 = f32[16,3,32,192]{3,2,1,0:T(8,128)} custom-call(bf16[16,3,32,192]{3,2,1,0:T(8,128)(2,1)} %bitcast.7, s32[48,32]{1,0:T(8,128)} %copy.12.missing, s32[1,32]{1,0:T(1,128)} %bitcast.11, f32[64,192]{1,0:T(8,128)} %feat_table.1, f32[1,192]{1,0:T(1,128)} %bitcast.8, f32[1,192]{1,0:T(1,128)} %bitcast.9, bf16[192,576]{1,0:T(8,128)(2,1)} %w_qkv.1, ...), custom_call_target="tpu_custom_call" | custom-call | tf_op jit(solution)/shard_map/pallas_call | solution.py:170
  38.6 2.7 %copy.15 = f32[48,32,192]{2,1,0:T(8,128)} copy(f32[48,32,192]{2,1,0:T(8,128)} %bitcast.6) | data formatting | bytes 2359296

commit v2 on v1

--- a/solution.py
+++ b/solution.py
@@ -12,6 +12,7 @@
 MESH = pl.DeviceIdType.MESH
 F32 = jnp.float32
 BF16 = jnp.bfloat16
+LIMIT = 60 * 1024 * 1024
 
 
 def cell_norm(values, gain):
@@ -70,11 +71,12 @@
     return jnp.concatenate(outs, axis=0).T
 
 
-def kernel(
-    n, rows, feats, width, packed,
-    cells, missing, feat_ids, feat_table, nan_embed, gain_one, w_qkv, w_out, gain_two, w_up, w_down,
-    out, tok, got, ctx, back, wqv_t, send_sems, recv_sems,
-):
+def kernel(n, rows, feats, width, packed, *refs):
+    sources, refs = refs[:11], refs[11:]
+    out, held, refs = refs[0], refs[1:12], refs[12:]
+    tok, got, ctx, back, wqv_t, done, load_sems, send_sems, recv_sems, out_sems = refs
+    (cells, missing, feat_ids, feat_table, nan_embed) = held[:5]
+    (gain_one, w_qkv, w_out, gain_two, w_up, w_down) = held[5:]
     me = lax.axis_index("feat")
     barrier = pltpu.get_barrier_semaphore()
 
@@ -84,6 +86,15 @@
         return carry
 
     lax.fori_loop(1, n, greet, 0)
+
+    loads = [
+        pltpu.make_async_copy(source, target, load_sems.at[spot])
+        for spot, (source, target) in enumerate(zip(sources, held))
+    ]
+    for load in loads:
+        load.start()
+    for load in loads[:5]:
+        load.wait()
 
     ncat = feat_table.shape[0]
     hot = (lax.broadcasted_iota(jnp.int32, (ncat, feats), 0) == feat_ids[...]).astype(F32)
@@ -92,11 +103,19 @@
         precision=lax.Precision.HIGHEST, preferred_element_type=F32,
     )
     nan = nan_embed[...]
-    absent = missing[...].astype(F32)[:, :, None].reshape(n, rows, feats, 1)
-    for row in range(rows):
-        values = cells[:, row].astype(F32)
-        values = (values + absent[:, row] * nan[None] + femb[None]).astype(BF16)
-        tok[row] = pack(values, packed)
+    absent = missing[...].astype(F32)
+    for row in range(rows):
+        for peer in range(n):
+            spot = peer * rows + row
+            values = cells[peer, row].astype(F32)
+            values = (values + absent[:, spot : spot + 1] * nan + femb).astype(BF16)
+            tok[row, peer] = pack(values, packed)
+    for row in range(rows):
+        got[row, pl.ds(me, 1)] = tok[row, pl.ds(me, 1)]
+    for load in loads[5:]:
+        load.wait()
+    wqv_t[0:width] = w_qkv[:, :width].astype(F32).T.astype(BF16)
+    wqv_t[width:] = w_qkv[:, 2 * width :].astype(F32).T.astype(BF16)
 
     pl.semaphore_wait(barrier, n - 1)
 
@@ -121,10 +140,6 @@
 
     for row in range(rows):
         spread(tok, got, 0, row)
-    for row in range(rows):
-        got[row, pl.ds(me, 1)] = tok[row, pl.ds(me, 1)]
-    wqv_t[0:width] = w_qkv[:, :width].astype(F32).T.astype(BF16)
-    wqv_t[width:] = w_qkv[:, 2 * width :].astype(F32).T.astype(BF16)
 
     def attention(row, carry):
         settle(got, recv_sems, 0, row)
@@ -139,6 +154,9 @@
 
     lax.fori_loop(0, rows, attention, 0)
 
+    def store(row):
+        return pltpu.make_async_copy(done.at[row], out.at[:, row], out_sems.at[row])
+
     def finish(row, carry):
         settle(back, recv_sems, 1, row)
         context = unpack(back[row].astype(F32), feats, width, packed).astype(BF16)
@@ -147,8 +165,11 @@
         normed = cell_norm(mid, gain_two[...])
         hidden = jnp.dot(normed, w_up[...], preferred_element_type=F32)
         act = (0.5 * hidden * (1.0 + lax.erf(hidden * math.sqrt(0.5)))).astype(BF16)
-        result = mid + jnp.dot(act, w_down[...], preferred_element_type=F32)
-        out[:, pl.ds(row, 1)] = result.reshape(n, 1, feats, width)
+        result = mid + lax.dot_general(
+            act, w_down[...], (((1,), (1,)), ((), ())), preferred_element_type=F32
+        )
+        done[row] = result.reshape(n, feats, width)
+        store(row).start()
         return carry
 
     lax.fori_loop(0, rows, finish, 0)
@@ -156,6 +177,7 @@
     for row in range(rows):
         settle(tok, send_sems, 0, row)
         settle(ctx, send_sems, 1, row)
+        store(row).wait()
 
 
 def body(
@@ -167,26 +189,9 @@
     packed = width == 192 and feats % 32 == 0
     piece = (feats + feats // 2, 128) if packed else (feats, width)
     buffer = pltpu.VMEM((rows, n) + piece, BF16)
-    result = pl.pallas_call(
-        functools.partial(kernel, n, rows, feats, width, packed),
-        out_shape=jax.ShapeDtypeStruct((n, rows, feats, width), F32),
-        in_specs=[pl.BlockSpec(memory_space=pltpu.VMEM)] * 11,
-        out_specs=pl.BlockSpec(memory_space=pltpu.VMEM),
-        scratch_shapes=[
-            buffer,
-            buffer,
-            buffer,
-            buffer,
-            pltpu.VMEM((2 * width, width), BF16),
-            pltpu.SemaphoreType.DMA((2, rows)),
-            pltpu.SemaphoreType.DMA((2, rows)),
-        ],
-        compiler_params=pltpu.CompilerParams(
-            collective_id=0, has_side_effects=True, vmem_limit_bytes=60 * 1024 * 1024
-        ),
-    )(
+    operands = (
         cells.reshape(n, rows, feats, width),
-        missing,
+        missing.T,
         feat_ids[None],
         feat_table,
         nan_embed[None],
@@ -195,8 +200,30 @@
         w_out,
         gain_two[None],
         w_up,
-        w_down,
+        w_down.T,
     )
+    result = pl.pallas_call(
+        functools.partial(kernel, n, rows, feats, width, packed),
+        out_shape=jax.ShapeDtypeStruct((n, rows, feats, width), F32),
+        in_specs=[pl.BlockSpec(memory_space=pltpu.HBM)] * len(operands),
+        out_specs=pl.BlockSpec(memory_space=pltpu.HBM),
+        scratch_shapes=[pltpu.VMEM(x.shape, x.dtype) for x in operands]
+        + [
+            buffer,
+            buffer,
+            buffer,
+            buffer,
+            pltpu.VMEM((2 * width, width), BF16),
+            pltpu.VMEM((rows, n, feats, width), F32),
+            pltpu.SemaphoreType.DMA((len(operands),)),
+            pltpu.SemaphoreType.DMA((2, rows)),
+            pltpu.SemaphoreType.DMA((2, rows)),
+            pltpu.SemaphoreType.DMA((rows,)),
+        ],
+        compiler_params=pltpu.CompilerParams(
+            collective_id=0, has_side_effects=True, vmem_limit_bytes=LIMIT
+        ),
+    )(*operands)
     return result.reshape(all_rows, feats, width)
 
 

time: 41.6 us -> 37.2 us (0.89)
  local copies, waits for them, and re-layouts: 6 us -> 2.73 us
  Pallas kernels: 35.3 us -> 34.3 us
    unnamed x3 -> x1, local copies, waits for them, and re-layouts: 6 us -> 2.73 us
    pallas_call x1, Pallas kernels: 35.3 us -> 34.3 us  [body(): pl.pallas_call(functools.partial(kernel, n, rows, feats, width, packed),...]
where the time goes in v2:
time: 37.2 us; the launch traced here: 37 us
  Pallas kernels  34.3 us (92%)
  local copies, waits for them, and re-layouts  2.73 us (7%)
    pallas_call x1, Pallas kernels, body(): pl.pallas_call(functools.partial(kernel, n, rows, feats, width, packed),...  34.3 us
    unnamed x1, local copies, waits for them, and re-layouts  2.73 us

profile of v2, /device:TPU:0, one launch (start us, length us, event | category | flops | bytes accessed | tf_op | source)
XLA Modules:
  0.0 37.0 jit_solution(8707216664696521903)
XLA Ops:
  0.0 34.3 %shard_map.109 = f32[16,3,32,192]{3,2,1,0:T(8,128)} custom-call(bf16[16,3,32,192]{3,2,1,0:T(8,128)(2,1)} %bitcast.9, s32[32,48]{1,0:T(8,128)} %bitcast.11, s32[1,32]{1,0:T(1,128)} %bitcast.15, f32[64,192]{1,0:T(8,128)} %refs_3_.1, f32[1,192]{1,0:T(1,128)} %bitcast.12, f32[1,192]{1,0:T(1,128)} %bitcast.13, bf16[192,576]{1,0:T(8,128)(2,1)} %refs_6_.1, ...), custom_call_target="tpu_custom_call" | custom-call | tf_op jit(solution)/shard_map/pallas_call | solution.py:205
  34.3 2.7 %copy.13 = f32[48,32,192]{2,1,0:T(8,128)} copy(f32[48,32,192]{2,1,0:T(8,128)} %bitcast.8) | data formatting | bytes 2359296

commit v3 on v2

--- a/solution.py
+++ b/solution.py
@@ -104,21 +104,6 @@
     )
     nan = nan_embed[...]
     absent = missing[...].astype(F32)
-    for row in range(rows):
-        for peer in range(n):
-            spot = peer * rows + row
-            values = cells[peer, row].astype(F32)
-            values = (values + absent[:, spot : spot + 1] * nan + femb).astype(BF16)
-            tok[row, peer] = pack(values, packed)
-    for row in range(rows):
-        got[row, pl.ds(me, 1)] = tok[row, pl.ds(me, 1)]
-    for load in loads[5:]:
-        load.wait()
-    wqv_t[0:width] = w_qkv[:, :width].astype(F32).T.astype(BF16)
-    wqv_t[width:] = w_qkv[:, 2 * width :].astype(F32).T.astype(BF16)
-
-    pl.semaphore_wait(barrier, n - 1)
-
     def spread(source, target, kind, row):
         def one(step, carry):
             peer = lax.rem(me + step, n)
@@ -139,7 +124,20 @@
         pltpu.make_async_copy(piece, piece, sems.at[kind, row]).wait()
 
     for row in range(rows):
+        for peer in range(n):
+            spot = peer * rows + row
+            values = cells[peer, row].astype(F32)
+            values = (values + absent[:, spot : spot + 1] * nan + femb).astype(BF16)
+            tok[row, peer] = pack(values, packed)
+        if row == 0:
+            pl.semaphore_wait(barrier, n - 1)
         spread(tok, got, 0, row)
+    for row in range(rows):
+        got[row, pl.ds(me, 1)] = tok[row, pl.ds(me, 1)]
+    for load in loads[5:]:
+        load.wait()
+    wqv_t[0:width] = w_qkv[:, :width].astype(F32).T.astype(BF16)
+    wqv_t[width:] = w_qkv[:, 2 * width :].astype(F32).T.astype(BF16)
 
     def attention(row, carry):
         settle(got, recv_sems, 0, row)

time: 37.2 us -> 36.4 us (0.978)
  Pallas kernels: 34.3 us -> 33.5 us
    pallas_call x1, Pallas kernels: 34.3 us -> 33.5 us  [body(): pl.pallas_call(functools.partial(kernel, n, rows, feats, width, packed),...]
where the time goes in v3:
time: 36.4 us; the launch traced here: 36.2 us
  Pallas kernels  33.5 us (92%)
  local copies, waits for them, and re-layouts  2.73 us (8%)
    pallas_call x1, Pallas kernels, body(): pl.pallas_call(functools.partial(kernel, n, rows, feats, width, packed),...  33.5 us
    unnamed x1, local copies, waits for them, and re-layouts  2.73 us

profile of v3, /device:TPU:0, one launch (start us, length us, event | category | flops | bytes accessed | tf_op | source)
XLA Modules:
  0.0 36.2 jit_solution(15683318160216526523)
XLA Ops:
  0.0 33.5 %shard_map.109 = f32[16,3,32,192]{3,2,1,0:T(8,128)} custom-call(bf16[16,3,32,192]{3,2,1,0:T(8,128)(2,1)} %bitcast.9, s32[32,48]{1,0:T(8,128)} %bitcast.11, s32[1,32]{1,0:T(1,128)} %bitcast.15, f32[64,192]{1,0:T(8,128)} %refs_3_.1, f32[1,192]{1,0:T(1,128)} %bitcast.12, f32[1,192]{1,0:T(1,128)} %bitcast.13, bf16[192,576]{1,0:T(8,128)(2,1)} %refs_6_.1, ...), custom_call_target="tpu_custom_call" | custom-call | tf_op jit(solution)/shard_map/pallas_call | solution.py:203
  33.5 2.7 %copy.13 = f32[48,32,192]{2,1,0:T(8,128)} copy(f32[48,32,192]{2,1,0:T(8,128)} %bitcast.8) | data formatting | bytes 2359296
